TPU v7x, 32 devices: a whole 2x2x4 slice. The times are simulated.
32 devices in a mesh: param: 16 (over z, y, x), sensor: 2 (over core).
Axes of the slice: x: 2, y: 2, z: 4, core: 2. Of those that a mesh axis runs over, the one named last changes fastest.
Arguments:
- data: float32 [16, 512, 420], P(None, ('sensor', 'param')), may hold values from -6 to 6
- spectra: float32 [2, 512, 64, 421], P(None, 'sensor', 'param'), may hold values from -2 to 2
Outputs:
- gradient: float32 [16, 64, 420], P(None, 'param')
- rms: float32 [16], replicated
All inputs are finite; a program needn't handle non-finite values.
Results may differ from a plain program's by a relative error of at most 0.0003.
Values sent between devices are 32-bit elements; how exact they have to be, the bound alone decides.
A program may use at most 128 MiB of HBM per device.

v0:
```python
import math
import jax
import jax.numpy as jnp
from jax import lax
from jax.sharding import PartitionSpec as P


def spectral_tables(steps):
    length = 2 * steps
    freqs = steps + 1
    times = lax.broadcasted_iota(jnp.int32, (steps, freqs), 0)
    bins = lax.broadcasted_iota(jnp.int32, (steps, freqs), 1)
    phase = 2.0 * math.pi / length * (times * bins % length).astype(jnp.float32)
    forward = jnp.concatenate([jnp.cos(phase), -jnp.sin(phase)], axis=1)
    weight = jnp.where((bins == 0) | (bins == steps), 1.0, 2.0) / length
    backward = jnp.concatenate([(weight * jnp.cos(phase)).T, (-weight * jnp.sin(phase)).T], axis=0)
    return (forward, backward)


def to_spectrum(series, forward):
    vectors, sensors, steps = series.shape
    flat = jnp.dot(
        series.reshape(vectors * sensors, steps),
        forward,
        precision=lax.Precision.HIGHEST,
        preferred_element_type=jnp.float32,
    )
    return flat.reshape(vectors, sensors, forward.shape[1])


def contract(kernel, spectrum):
    return jnp.einsum(
        "spf,rsf->rpf",
        kernel,
        spectrum,
        precision=lax.Precision.HIGHEST,
        preferred_element_type=jnp.float32,
    )


def body(data, spectra):
    steps = data.shape[2]
    freqs = steps + 1
    forward, backward = spectral_tables(steps)
    whole = to_spectrum(lax.all_gather(data, "param", axis=1, tiled=True), forward)
    real_part = whole[..., :freqs]
    imag_part = whole[..., freqs:]
    kernel_re = spectra[0]
    kernel_im = spectra[1]
    out_re = contract(kernel_re, real_part) + contract(kernel_im, imag_part)
    out_im = contract(kernel_re, imag_part) - contract(kernel_im, real_part)
    vectors, points = (out_re.shape[0], out_re.shape[1])
    stacked = jnp.concatenate([out_re, out_im], axis=2).reshape(vectors * points, 2 * freqs)
    partial_field = jnp.dot(
        stacked, backward, precision=lax.Precision.HIGHEST, preferred_element_type=jnp.float32
    ).reshape(vectors, points, steps)
    count = points * lax.axis_size("param") * steps
    share = lax.psum_scatter(partial_field, "sensor", scatter_dimension=0, tiled=True)
    squares = lax.psum(jnp.sum(share * share, axis=(1, 2)), "param")
    scale = jnp.sqrt(squares / count + 1e-06)
    normalized = share / scale[:, None, None]
    gradient, rms_all = (
        lax.all_gather(normalized, "sensor", axis=0, tiled=True),
        lax.all_gather(scale, "sensor", axis=0, tiled=True),
    )
    return (gradient, rms_all)


def solution(mesh):
    in_specs = (P(None, ("sensor", "param"), None), P(None, "sensor", "param", None))
    out_specs = (P(None, "param", None), P())
    return jax.shard_map(body, mesh=mesh, in_specs=in_specs, out_specs=out_specs, check_vma=False)
```

profile of v0, /device:TPU:0, one launch (start us, length us, event | category | flops | bytes accessed | tf_op | source)
XLA Modules:
  0.0 326.7 jit_solution(8645191133042081712)
XLA Ops:
  8.0 4.5 %sine_negate_fusion = (f32[420,421]{1,0:T(8,128)}, f32[420,421]{1,0:T(8,128)}) fusion(), kind=kLoop, calls=%fused_computation.39 | loop fusion | flops 1768200 | bytes 1414560 | tf_op jit(solution)/shard_map/neg | solution.py:14
  12.5 4.6 %sine_multiply_fusion = (f32[421,420]{0,1:T(8,128)}, f32[421,420]{0,1:T(8,128)}) fusion(f32[421]{0:T(512)S(1)} %fusion.42, f32[421]{0:T(512)S(1)} %select_multiply_fusion), kind=kLoop, calls=%fused_computation.34 | loop fusion | flops 1945020 | bytes 1417928 | tf_op jit(solution)/shard_map/mul | solution.py:16
  17.0 1.5 fusion.73
  18.5 1.5 fusion.71
  20.0 1.5 fusion.75
  21.6 1.5 fusion.77
  23.1 102.6 %all-gather.2.cloned.1.call-done = f32[16,256,420]{2,1,0:T(8,128)} async-done(((f32[16,16,420]{2,1,0:T(8,128)}), f32[16,256,420]{2,1,0:T(8,128)}) %all-gather.2.cloned.1.call-update) | async-done | bytes 6881296 | tf_op jit(solution)/shard_map/all_gather | solution.py:45
  125.7 51.7 %fusion.20 = f32[842,4096]{1,0:T(8,128)} fusion(f32[4096,420]{1,0:T(8,128)} %bitcast.71, f32[420,421]{1,0:T(8,128)} %get-tuple-element.6, f32[420,421]{1,0:T(8,128)} %get-tuple-element.7), kind=kOutput, calls=%fused_computation.20 | convolution fusion | flops 17382467584 | bytes 22091168 | tf_op jit(solution)/shard_map/dot_general | solution.py:22
  177.4 16.8 %copy.9 = f32[106,8,16,256]{3,2,1,0:T(8,128)} copy(f32[106,8,16,256]{3,1,2,0:T(8,128)} %bitcast.70) | data formatting | bytes 27787264
  194.2 14.2 %fusion.2 = f32[421,16,4]{1,2,0:T(4,128)} fusion(f32[848,16,256]{2,1,0:T(8,128)} %bitcast.66, f32[256,4,421]{0,1,2:T(4,128)S(1)} %copy-done.4), kind=kOutput, calls=%fused_computation.2 | convolution fusion | flops 82771968 | bytes 15627520 | tf_op jit(solution)/shard_map/spf,rsf->rpf/dot_general | solution.py:32
  208.5 2.1 copy.5
  210.6 14.2 %fusion = f32[421,16,4]{1,2,0:T(4,128)} fusion(f32[848,16,256]{2,1,0:T(8,128)} %bitcast.67, f32[256,4,421]{0,1,2:T(4,128)S(1)} %copy-done.3), kind=kOutput, calls=%fused_computation | convolution fusion | flops 82771968 | bytes 15627520 | tf_op jit(solution)/shard_map/spf,rsf->rpf/dot_general | solution.py:32
  224.8 2.1 copy.6
  226.9 14.3 %fusion.4 = f32[421,16,4]{1,2,0:T(4,128)} fusion(f32[848,16,256]{2,1,0:T(8,128)} %bitcast.68, f32[256,4,421]{0,1,2:T(4,128)S(1)} %copy-done.2), kind=kOutput, calls=%fused_computation.4 | convolution fusion | flops 82771968 | bytes 15627520 | tf_op jit(solution)/shard_map/spf,rsf->rpf/dot_general | solution.py:32
  241.2 2.1 copy.7
  243.3 14.1 %fusion.6 = f32[421,16,4]{1,2,0:T(4,128)} fusion(f32[848,16,256]{2,1,0:T(8,128)} %bitcast.69, f32[256,4,421]{0,1,2:T(4,128)S(1)} %copy-done.1), kind=kOutput, calls=%fused_computation.6 | convolution fusion | flops 82771968 | bytes 15627520 | tf_op jit(solution)/shard_map/spf,rsf->rpf/dot_general | solution.py:32
  257.4 1.5 copy.8
  258.9 1.0 add_bitcast_fusion
  260.8 2.3 fusion.24
  263.7 5.8 %reduce-scatter.2.cloned.1.call-done = f32[8,4,420]{2,0,1:T(8,128)} async-done(((f32[16,4,420]{2,0,1:T(8,128)}), f32[8,4,420]{2,0,1:T(8,128)}) %reduce-scatter.2.cloned.1.call-update) | async-done | bytes 53776 | tf_op jit(solution)/shard_map/reduce_scatter | solution.py:58
  269.5 1.0 multiply_reduce_fusion
  271.1 41.9 %psum.7 = f32[8]{0:T(128)S(1)} all-reduce(f32[8]{0:T(128)S(1)} %multiply_reduce_fusion), channel_id=1, replica_groups=mesh['param'=16,'sensor'=2] {'param'}, use_global_device_ids=true, to_apply=%region_2.3 | all-reduce | flops 8 | bytes 64 | tf_op jit(solution)/shard_map/psum | solution.py:59
  314.0 1.9 all_gather.10
  316.7 2.9 all-reduce
  (28 shorter events, 4.1 us)
Async XLA Ops:
  7.2 9.9 %copy-start = (f32[2,256,4,421]{1,2,3,0:T(4,128)S(1)}, f32[2,256,4,421]{1,2,3,0:T(4,128)}, u32[]{:S(2)}) copy-start(f32[2,256,4,421]{1,2,3,0:T(4,128)} %param.3) | copy-start | bytes 10346500
  7.2 118.6 %all-gather.2.cloned.1.call-start = ((), (), s32[]{:S(2)}) async-start(), calls=%async_computation.1 | async-start | bytes 8912896 | tf_op jit(solution)/shard_map/all_gather | solution.py:45
  7.9 261.6 %reduce-scatter.2.cloned.1.call-start = ((), (), s32[]{:S(2)}) async-start(), calls=%async_computation.2 | async-start | bytes 196608 | tf_op jit(solution)/shard_map/reduce_scatter | solution.py:58
  177.4 16.8 %copy-start.4 = (f32[256,4,421]{0,1,2:T(4,128)S(1)}, f32[256,4,421]{0,1,2:T(4,128)}, u32[]{:S(2)}) copy-start(f32[256,4,421]{0,1,2:T(4,128)} %fusion.73) | copy-start | bytes 5173252
  194.2 16.3 %copy-start.3 = (f32[256,4,421]{0,1,2:T(4,128)S(1)}, f32[256,4,421]{0,1,2:T(4,128)}, u32[]{:S(2)}) copy-start(f32[256,4,421]{0,1,2:T(4,128)} %fusion.71) | copy-start | bytes 5173252
  210.6 16.3 %copy-start.2 = (f32[256,4,421]{0,1,2:T(4,128)S(1)}, f32[256,4,421]{0,1,2:T(4,128)}, u32[]{:S(2)}) copy-start(f32[256,4,421]{0,1,2:T(4,128)} %fusion.75) | copy-start | bytes 5173252
  226.9 16.4 %copy-start.1 = (f32[256,4,421]{0,1,2:T(4,128)S(1)}, f32[256,4,421]{0,1,2:T(4,128)}, u32[]{:S(2)}) copy-start(f32[256,4,421]{0,1,2:T(4,128)} %fusion.77) | copy-start | bytes 5173252
  243.3 17.5 %copy-start.5 = (f32[421,420]{0,1:T(8,128)S(1)}, f32[421,420]{0,1:T(8,128)}, u32[]{:S(2)}) copy-start(f32[421,420]{0,1:T(8,128)} %get-tuple-element.8) | copy-start | bytes 2121844
  243.3 17.5 %copy-start.6 = (f32[421,420]{0,1:T(8,128)S(1)}, f32[421,420]{0,1:T(8,128)}, u32[]{:S(2)}) copy-start(f32[421,420]{0,1:T(8,128)} %get-tuple-element.9) | copy-start | bytes 2121844
  257.4 5.7 %copy-start.7 = (u32[32]{0:T(128)S(1)}, u32[32]{0:T(128)}, u32[]{:S(2)}) copy-start(u32[32]{0:T(128)} %constant.35) | copy-start | bytes 388
Sparse Core Ops, SparseCore 0:
  10.8 114.9 all-gather.1
  263.2 6.2 reduce-scatter.1
where the time goes:
time: 330 us; the launch traced here: 327 us
  matrix products  111 us (34%)
  waiting for transfers between devices  109 us (33%)
  blocking collectives  46.8 us (14%)
  local copies, waits for them, and re-layouts  32 us (10%)
  between operations  15 us (5%)
  other arithmetic  13 us (4%)
    all_gather x1, waiting for transfers between devices, body(): lax.all_gather(data, 'param', axis=1, tiled=True)  103 us
    dot_general x4, matrix products, contract(): jnp.einsum('spf,rsf->rpf', kernel, spectrum, precision=lax.Precision.HIGH...  56.8 us
    dot_general x1, matrix products, to_spectrum(): jnp.dot(series.reshape(vectors * sensors, steps), forward, precision=lax....  51.7 us
    psum x1, blocking collectives, body(): squares = lax.psum(jnp.sum(share * share, axis=(1, 2)), 'param')  41.9 us
    unnamed x20, local copies, waits for them, and re-layouts  18.2 us
    dot_general x8, local copies, waits for them, and re-layouts, contract(): jnp.einsum('spf,rsf->rpf', kernel, spectrum, precision=lax.Precision.HIGH...  13.8 us
  transfers between devices with their start and end apart: 2, of which 2 were waited for; matrix products, arithmetic and copies ran while one was open for 5% of the time, Pallas kernels for 0%

commit v1 on v0

--- a/solution.py
+++ b/solution.py
@@ -56,7 +56,7 @@
     ).reshape(vectors, points, steps)
     count = points * lax.axis_size("param") * steps
     share = lax.psum_scatter(partial_field, "sensor", scatter_dimension=0, tiled=True)
-    squares = lax.psum(jnp.sum(share * share, axis=(1, 2)), "param")
+    squares = jnp.sum(lax.all_gather(jnp.sum(share * share, axis=(1, 2)), "param"), axis=0)
     scale = jnp.sqrt(squares / count + 1e-06)
     normalized = share / scale[:, None, None]
     gradient, rms_all = (

time: 330 us -> 330 us (level)
    psum x1 -> x0, blocking collectives: 41.9 us -> none  [body(): squares = lax.psum(jnp.sum(share * share, axis=(1, 2)), 'param')]
    unnamed x1 -> x2, blocking collectives: 2.95 us -> 44.8 us
    unnamed x20 -> x25, local copies, waits for them, and re-layouts: 18.2 us -> 19 us
where the time goes in v1:
time: 330 us; the launch traced here: 327 us
  matrix products  111 us (34%)
  waiting for transfers between devices  107 us (32%)
  blocking collectives  46.7 us (14%)
  local copies, waits for them, and re-layouts  32.9 us (10%)
  between operations  15.6 us (5%)
  other arithmetic  13 us (4%)
    all_gather x1, waiting for transfers between devices, body(): lax.all_gather(data, 'param', axis=1, tiled=True)  103 us
    dot_general x4, matrix products, contract(): jnp.einsum('spf,rsf->rpf', kernel, spectrum, precision=lax.Precision.HIGH...  57.1 us
    dot_general x1, matrix products, to_spectrum(): jnp.dot(series.reshape(vectors * sensors, steps), forward, precision=lax....  51.8 us
    unnamed x2, blocking collectives  44.8 us
    unnamed x25, local copies, waits for them, and re-layouts  19 us
    dot_general x8, local copies, waits for them, and re-layouts, contract(): jnp.einsum('spf,rsf->rpf', kernel, spectrum, precision=lax.Precision.HIGH...  13.9 us
  transfers between devices with their start and end apart: 2, of which 2 were waited for; matrix products, arithmetic and copies ran while one was open for 5% of the time, Pallas kernels for 0%

profile of v1, /device:TPU:0, one launch (start us, length us, event | category | flops | bytes accessed | tf_op | source)
XLA Modules:
  0.0 326.8 jit_solution(10763029362317359491)
XLA Ops:
  8.0 4.5 %sine_negate_fusion = (f32[420,421]{1,0:T(8,128)}, f32[420,421]{1,0:T(8,128)}) fusion(), kind=kLoop, calls=%fused_computation.39 | loop fusion | flops 1768200 | bytes 1414560 | tf_op jit(solution)/shard_map/neg | solution.py:14
  12.5 4.6 %sine_multiply_fusion = (f32[421,420]{0,1:T(8,128)}, f32[421,420]{0,1:T(8,128)}) fusion(f32[421]{0:T(512)S(1)} %fusion.42, f32[421]{0:T(512)S(1)} %select_multiply_fusion), kind=kLoop, calls=%fused_computation.34 | loop fusion | flops 1945020 | bytes 1417928 | tf_op jit(solution)/shard_map/mul | solution.py:16
  17.1 1.5 fusion.73
  18.6 1.5 fusion.71
  20.1 1.5 fusion.75
  21.6 1.5 fusion.77
  23.1 102.6 %all-gather.3.cloned.1.call-done = f32[16,256,420]{2,1,0:T(8,128)} async-done(((f32[16,16,420]{2,1,0:T(8,128)}), f32[16,256,420]{2,1,0:T(8,128)}) %all-gather.3.cloned.1.call-update) | async-done | bytes 6881296 | tf_op jit(solution)/shard_map/all_gather | solution.py:45
  125.7 51.8 %fusion.20 = f32[842,4096]{1,0:T(8,128)} fusion(f32[4096,420]{1,0:T(8,128)} %bitcast.72, f32[420,421]{1,0:T(8,128)} %get-tuple-element.8, f32[420,421]{1,0:T(8,128)} %get-tuple-element.9), kind=kOutput, calls=%fused_computation.20 | convolution fusion | flops 17382467584 | bytes 22091168 | tf_op jit(solution)/shard_map/dot_general | solution.py:22
  177.5 16.8 %copy.10 = f32[106,8,16,256]{3,2,1,0:T(8,128)} copy(f32[106,8,16,256]{3,1,2,0:T(8,128)} %bitcast.71) | data formatting | bytes 27787264
  194.3 14.2 %fusion.2 = f32[421,16,4]{1,2,0:T(4,128)} fusion(f32[848,16,256]{2,1,0:T(8,128)} %bitcast.67, f32[256,4,421]{0,1,2:T(4,128)S(1)} %copy-done.4), kind=kOutput, calls=%fused_computation.2 | convolution fusion | flops 82771968 | bytes 15627520 | tf_op jit(solution)/shard_map/spf,rsf->rpf/dot_general | solution.py:32
  208.6 2.1 copy.6
  210.7 14.2 %fusion = f32[421,16,4]{1,2,0:T(4,128)} fusion(f32[848,16,256]{2,1,0:T(8,128)} %bitcast.68, f32[256,4,421]{0,1,2:T(4,128)S(1)} %copy-done.3), kind=kOutput, calls=%fused_computation | convolution fusion | flops 82771968 | bytes 15627520 | tf_op jit(solution)/shard_map/spf,rsf->rpf/dot_general | solution.py:32
  224.9 2.1 copy.7
  227.0 14.3 %fusion.4 = f32[421,16,4]{1,2,0:T(4,128)} fusion(f32[848,16,256]{2,1,0:T(8,128)} %bitcast.69, f32[256,4,421]{0,1,2:T(4,128)S(1)} %copy-done.2), kind=kOutput, calls=%fused_computation.4 | convolution fusion | flops 82771968 | bytes 15627520 | tf_op jit(solution)/shard_map/spf,rsf->rpf/dot_general | solution.py:32
  241.3 2.1 copy.8
  243.4 14.3 %fusion.6 = f32[421,16,4]{1,2,0:T(4,128)} fusion(f32[848,16,256]{2,1,0:T(8,128)} %bitcast.70, f32[256,4,421]{0,1,2:T(4,128)S(1)} %copy-done.1), kind=kOutput, calls=%fused_computation.6 | convolution fusion | flops 82771968 | bytes 15627520 | tf_op jit(solution)/shard_map/spf,rsf->rpf/dot_general | solution.py:32
  257.8 1.5 copy.9
  259.3 1.0 add_bitcast_fusion
  261.2 2.3 fusion.24
  265.9 4.0 %reduce-scatter.2.cloned.1.call-done = f32[8,4,420]{2,0,1:T(8,128)} async-done(((f32[16,4,420]{2,0,1:T(8,128)}), f32[8,4,420]{2,0,1:T(8,128)}) %reduce-scatter.2.cloned.1.call-update) | async-done | bytes 53776 | tf_op jit(solution)/shard_map/reduce_scatter | solution.py:58
  269.9 1.0 multiply_reduce_fusion
  271.1 41.9 %all-reduce = f32[128]{0:T(128)S(1)} all-reduce(f32[128]{0:T(128)S(1)} %dynamic-update-slice), channel_id=2, replica_groups=mesh['param'=16,'sensor'=2] {'param'}, use_global_device_ids=true, to_apply=%add | all-reduce | flops 128 | bytes 1024
  314.1 1.9 all_gather.18
  316.8 2.9 all-reduce.1
  (35 shorter events, 5.0 us)
Async XLA Ops:
  7.2 9.9 %copy-start = (f32[2,256,4,421]{1,2,3,0:T(4,128)S(1)}, f32[2,256,4,421]{1,2,3,0:T(4,128)}, u32[]{:S(2)}) copy-start(f32[2,256,4,421]{1,2,3,0:T(4,128)} %param.3) | copy-start | bytes 10346500
  7.2 118.6 %all-gather.3.cloned.1.call-start = ((), (), s32[]{:S(2)}) async-start(), calls=%async_computation.1 | async-start | bytes 8912896 | tf_op jit(solution)/shard_map/all_gather | solution.py:45
  7.9 262.0 %reduce-scatter.2.cloned.1.call-start = ((), (), s32[]{:S(2)}) async-start(), calls=%async_computation.2 | async-start | bytes 196608 | tf_op jit(solution)/shard_map/reduce_scatter | solution.py:58
  177.5 16.8 %copy-start.4 = (f32[256,4,421]{0,1,2:T(4,128)S(1)}, f32[256,4,421]{0,1,2:T(4,128)}, u32[]{:S(2)}) copy-start(f32[256,4,421]{0,1,2:T(4,128)} %fusion.73) | copy-start | bytes 5173252
  194.3 16.3 %copy-start.3 = (f32[256,4,421]{0,1,2:T(4,128)S(1)}, f32[256,4,421]{0,1,2:T(4,128)}, u32[]{:S(2)}) copy-start(f32[256,4,421]{0,1,2:T(4,128)} %fusion.71) | copy-start | bytes 5173252
  210.7 16.3 %copy-start.2 = (f32[256,4,421]{0,1,2:T(4,128)S(1)}, f32[256,4,421]{0,1,2:T(4,128)}, u32[]{:S(2)}) copy-start(f32[256,4,421]{0,1,2:T(4,128)} %fusion.75) | copy-start | bytes 5173252
  227.0 16.4 %copy-start.1 = (f32[256,4,421]{0,1,2:T(4,128)S(1)}, f32[256,4,421]{0,1,2:T(4,128)}, u32[]{:S(2)}) copy-start(f32[256,4,421]{0,1,2:T(4,128)} %fusion.77) | copy-start | bytes 5173252
  243.4 17.8 %copy-start.5 = (f32[421,420]{0,1:T(8,128)S(1)}, f32[421,420]{0,1:T(8,128)}, u32[]{:S(2)}) copy-start(f32[421,420]{0,1:T(8,128)} %get-tuple-element.10) | copy-start | bytes 2121844
  243.4 17.8 %copy-start.6 = (f32[421,420]{0,1:T(8,128)S(1)}, f32[421,420]{0,1:T(8,128)}, u32[]{:S(2)}) copy-start(f32[421,420]{0,1:T(8,128)} %get-tuple-element.11) | copy-start | bytes 2121844
  257.8 5.7 %copy-start.8 = (u32[32]{0:T(128)S(1)}, u32[32]{0:T(128)}, u32[]{:S(2)}) copy-start(u32[32]{0:T(128)} %constant.35) | copy-start | bytes 388
  257.8 6.3 %copy-start.7 = (u32[32]{0:T(128)S(1)}, u32[32]{0:T(128)}, u32[]{:S(2)}) copy-start(u32[32]{0:T(128)} %constant.40) | copy-start | bytes 388
Sparse Core Ops, SparseCore 0:
  10.8 114.9 all-gather.2
  263.6 6.2 reduce-scatter.1
